TPU v7x, 32 devices: a whole 2x2x4 slice. The times are simulated.
32 devices in a mesh: rep: 8 (over z, y), shard: 4 (over x, core).
Axes of the slice: x: 2, y: 2, z: 4, core: 2. Of those that a mesh axis runs over, the one named last changes fastest.
Arguments:
- activ: bfloat16 [4096, 8192], P(('rep', 'shard')), may hold values from -6 to 6
- key_grad: bfloat16 [4096, 640], P(('rep', 'shard')), may hold values from -1.1953125 to 1.1953125
- key_weight: bfloat16 [8192, 640], P('shard'), may hold values from -0.25 to 0.25
- feedback: bfloat16 [8, 40960, 128], P('rep', 'shard'), may hold values from -24 to 24
- kept: int32 [8, 4, 512], P('rep', 'shard'), may hold values from 0 to 10239, as said below
- region_len: int32 [4, 8], P('shard'), may hold values from 640 to 1920, as said below
Outputs:
- input_grad: bfloat16 [4096, 8192], P(('rep', 'shard'))
- next_feedback: bfloat16 [8, 40960, 128], P('rep', 'shard')
- owned_sum: float32 [4, 15360, 128], P('shard', 'rep')
Inputs may be any that keep to these rules, and one draw needn't show every extreme that they name: `region_len`: each row splits its shard's 10240 blocks into 8 regions in order of owner and sums to 10240; every row has a region of exactly 1920 blocks. `kept`: the 512 numbers of a row are different blocks of that shard. At most 128 of them lie in one region of the shard; every row has exactly 128 in some region, and in every shard some region gets exactly 128 from every replica.
All inputs are finite; a program needn't handle non-finite values.
Results may differ from a plain program's by a relative error of at most 0.011.
Values may be sent and summed in bfloat16 or wider, within the bound.
A program may use at most 128 MiB of HBM per device.

v0:
```python
import jax
import jax.numpy as jnp
from jax import lax
from jax.sharding import PartitionSpec as P


def accumulate(block_rows, block_ids, own_start, own_len, region_max):
    offset = block_ids - own_start
    inside = (offset >= 0) & (offset < own_len)
    target = jnp.where(inside, offset, region_max)
    blank = jnp.zeros((region_max, block_rows.shape[1]), jnp.float32)
    return blank.at[target].add(block_rows.astype(jnp.float32), mode="drop")


def per_device(activ, key_grad, key_weight, feedback, kept, region_len):
    grads_all = lax.all_gather(key_grad, "shard", axis=0, tiled=True)
    act_cols = lax.all_to_all(activ, "shard", split_axis=1, concat_axis=0, tiled=True)
    weight_grad = lax.dot_general(
        act_cols, grads_all, (((0,), (0,)), ((), ())), preferred_element_type=jnp.float32
    )
    input_cols = lax.dot_general(
        grads_all, key_weight, (((1,), (1,)), ((), ())), preferred_element_type=jnp.float32
    ).astype(jnp.bfloat16)
    input_grad = lax.all_to_all(input_cols, "shard", split_axis=0, concat_axis=1, tiled=True)
    table = feedback[0]
    chosen = kept[0, 0]
    lengths = region_len[0]
    replicas = lax.axis_size("rep")
    block_count = table.shape[0]
    block_size = table.shape[1]
    keep_count = chosen.shape[0]
    mean_len = block_count // replicas
    region_max = mean_len + mean_len // 2
    starts = jnp.cumsum(lengths) - lengths
    owner_self = lax.axis_index("rep")
    own_start = starts[owner_self]
    own_len = lengths[owner_self]
    kept_rows = table[chosen]
    flags = jnp.zeros((block_count,), bool).at[chosen].set(True)
    cleared = jnp.where(flags[:, None], jnp.float32(0.0), table.astype(jnp.float32))
    next_feedback = (cleared + weight_grad.reshape(block_count, block_size)).astype(jnp.bfloat16)[
        None
    ]
    owner_id = jnp.sum((starts[None, :] <= chosen[:, None]).astype(jnp.int32), axis=1) - 1
    serial = jnp.arange(keep_count, dtype=jnp.int32)
    earlier = (owner_id[:, None] == owner_id[None, :]) & (serial[None, :] < serial[:, None])
    slot_index = jnp.sum(earlier.astype(jnp.int32), axis=1)
    capacity = 2 * keep_count // replicas
    place_at = owner_id * capacity + slot_index
    send_rows = (
        jnp.zeros((replicas * capacity, block_size), jnp.bfloat16).at[place_at].set(kept_rows)
    )
    send_ids = jnp.full((replicas * capacity,), -1, jnp.int32).at[place_at].set(chosen)
    got_rows, got_ids = (
        lax.all_to_all(send_rows, "rep", split_axis=0, concat_axis=0, tiled=True),
        lax.all_to_all(send_ids, "rep", split_axis=0, concat_axis=0, tiled=True),
    )
    owned_rows = accumulate(got_rows, got_ids, own_start, own_len, region_max)
    return (input_grad, next_feedback, owned_rows[None])


def solution(mesh):
    return jax.shard_map(
        per_device,
        mesh=mesh,
        in_specs=(
            P(("rep", "shard"), None),
            P(("rep", "shard"), None),
            P("shard", None),
            P("rep", "shard", None),
            P("rep", "shard", None),
            P("shard", None),
        ),
        out_specs=(P(("rep", "shard"), None), P("rep", "shard", None), P("shard", "rep", None)),
        check_vma=False,
    )
```

profile of v0, /device:TPU:0, one launch (start us, length us, event | category | flops | bytes accessed | tf_op | source)
XLA Modules:
  0.0 117.7 jit_solution(1622688939139694994)
XLA Ops:
  0.6 0.0 copy-start
  0.6 1.0 reduce-window.4
  1.6 0.7 fusion.11
  2.3 0.8 convert_reduce_fusion.1
  3.1 0.3 convert_reduce_fusion
  3.3 3.2 %scatter_custom_fusion.1 = s32[1024]{0:T(1024)} fusion(s32[512]{0:T(512)S(1)} %bitcast.56, s32[512]{0:T(512)} %bitcast.54, s32[]{:T(128)} %constant.18.clone.1), kind=kCustom, calls=%fused_computation.26 | custom fusion | bytes 4608 | tf_op jit(solution)/shard_map/scatter | solution.py:53
  6.5 7.3 %all-to-all-start.2 = ((s32[8,128,1]{1,2,0:T(1,128)}), s32[8,128,1]{1,2,0:T(1,128)S(1)}, u32[]{:S(2)}, u32[]{:S(2)}) async-start(s32[8,128,1]{1,2,0:T(1,128)} %bitcast.14), calls=%async_computation.2 | async-start | bytes 8192 | tf_op jit(solution)/shard_map/all_to_all | solution.py:56
  13.8 0.7 compare_select_fusion.2
  14.5 0.0 copy-start.2
  14.5 0.6 copy-done.2
  15.1 5.5 %scatter_custom_fusion.2 = bf16[1024,128]{1,0:T(8,128)(2,1)} fusion(s32[512]{0:T(512)S(1)} %bitcast.57, bf16[]{:T(256)} %constant.12.clone.1, bf16[10240,128]{1,0:T(8,128)(2,1)} %bitcast.43, s32[1024]{0:T(1024)S(1)} %pad_clamp_fusion), kind=kCustom, calls=%fused_computation.13 | custom fusion | bytes 262656 | tf_op jit(solution)/shard_map/scatter | solution.py:51
  20.6 0.0 all-to-all-done.2
  20.6 6.0 %all-to-all-start.3 = ((bf16[8,128,128]{2,1,0:T(8,128)(2,1)}), bf16[8,128,128]{2,1,0:T(8,128)(2,1)S(1)}, u32[]{:S(2)}, u32[]{:S(2)}) async-start(bf16[8,128,128]{2,1,0:T(8,128)(2,1)} %bitcast.23), calls=%async_computation.3 | async-start | bytes 524288 | tf_op jit(solution)/shard_map/all_to_all | solution.py:55
  26.6 4.1 %copy.20 = bf16[128,8192]{0,1:T(8,128)(2,1)} copy(bf16[128,8192]{1,0:T(8,128)(2,1)} %param.6) | data formatting | bytes 4194304 | tf_op args[0]
  30.7 4.4 %all-to-all-done.3 = bf16[8,128,128]{2,1,0:T(8,128)(2,1)S(1)} async-done(((bf16[8,128,128]{2,1,0:T(8,128)(2,1)}), bf16[8,128,128]{2,1,0:T(8,128)(2,1)S(1)}, u32[]{:S(2)}, u32[]{:S(2)}) %all-to-all-start.3) | async-done | bytes 262176 | tf_op jit(solution)/shard_map/all_to_all | solution.py:55
  35.1 4.4 %all-to-all-start.1 = ((bf16[128,4,2048]{0,2,1:T(8,128)(2,1)}), bf16[128,4,2048]{0,2,1:T(8,128)(2,1)}, u32[]{:S(2)}, u32[]{:S(2)}) async-start(bf16[128,4,2048]{0,2,1:T(8,128)(2,1)} %bitcast.42), calls=%async_computation.1 | async-start | bytes 4194304 | tf_op jit(solution)/shard_map/all_to_all | solution.py:17
  39.6 30.0 %all_gather.3 = bf16[512,640]{1,0:T(8,128)(2,1)S(1)} all-gather(bf16[128,640]{1,0:T(8,128)(2,1)} %param.7), channel_id=1, replica_groups=mesh['rep'=8,'shard'=4] {'shard'}, dimensions={0}, use_global_device_ids=true | all-gather | bytes 819200 | tf_op jit(solution)/shard_map/all_gather | solution.py:16
  69.6 0.0 copy-done
  69.6 3.1 %convolution_convert_fusion = bf16[512,2048]{1,0:T(8,128)(2,1)} fusion(bf16[512,640]{1,0:T(8,128)(2,1)S(1)} %all_gather.3, bf16[2048,640]{1,0:T(8,128)(2,1)S(1)} %copy-done), kind=kOutput, calls=%fused_computation.6 | convolution fusion | flops 1343225856 | bytes 5373952 | tf_op jit(solution)/shard_map/dot_general | solution.py:21
  72.7 0.0 copy-start.3
  72.7 0.0 all-to-all-done.1
  72.7 4.6 %all-to-all-start = ((bf16[4,128,2048]{2,1,0:T(8,128)(2,1)}), bf16[4,128,2048]{2,1,0:T(8,128)(2,1)}, u32[]{:S(2)}, u32[]{:S(2)}) async-start(bf16[4,128,2048]{2,1,0:T(8,128)(2,1)} %bitcast.44), calls=%async_computation | async-start | bytes 4194304 | tf_op jit(solution)/shard_map/all_to_all | solution.py:24
  77.4 0.0 copy-done.3
  77.4 0.6 constant_dynamic-slice_fusion
  78.0 0.6 dynamic_slice.6
  78.6 0.5 broadcast.121
  79.1 2.6 %scatter_custom_fusion = pred[10240]{0:T(1024)(128)(4,1)S(1)} fusion(s32[512]{0:T(512)} %bitcast.51, pred[512]{0:T(512)(128)(4,1)} %broadcast.121, pred[]{:T(512)} %constant.13.clone.1), kind=kCustom, calls=%fused_computation.17 | custom fusion | bytes 10752 | tf_op jit(solution)/shard_map/scatter | solution.py:39
  81.7 0.7 broadcast_subtract_fusion
  82.3 0.6 compare_select_fusion
  83.0 7.0 %scatter_custom_fusion.3 = f32[1920,128]{1,0:T(8,128)} fusion(s32[1024]{0:T(1024)S(1)} %bitcast.55, bf16[1024,128]{1,0:T(8,128)(2,1)S(1)} %bitcast.46, f32[]{:T(128)} %constant.17.clone.1), kind=kCustom, calls=%fused_computation.10 | custom fusion | flops 262144 | bytes 1245188 | tf_op jit(solution)/shard_map/scatter-add | solution.py:12
  90.0 3.9 %copy.21 = bf16[4,128,2048]{2,1,0:T(8,128)(2,1)} copy(bf16[4,128,2048]{1,2,0:T(8,128)(2,1)} %bitcast.5) | data formatting | bytes 4194304 | tf_op jit(solution)/shard_map/all_to_all | solution.py:17
  93.9 5.8 %fusion.12 = f32[2048,640]{1,0:T(8,128)} fusion(bf16[512,2048]{1,0:T(8,128)(2,1)} %bitcast.41, bf16[512,640]{1,0:T(8,128)(2,1)S(1)} %all_gather.3), kind=kOutput, calls=%fused_computation.33 | convolution fusion | flops 1342177280 | bytes 7995392 | tf_op jit(solution)/shard_map/dot_general | solution.py:18
  99.7 6.5 %reshape.138 = f32[1,10240,128]{2,1,0:T(8,128)} reshape(f32[2048,640]{1,0:T(8,128)} %fusion.12) | data formatting | bytes 10485760 | tf_op jit(solution)/shard_map/reshape | solution.py:41
  106.2 0.0 all-to-all-done
  106.2 0.0 copy-start.1
  106.2 3.3 %copy.24 = bf16[4,16,8,2048]{3,2,0,1:T(8,128)(2,1)} copy(bf16[4,16,8,2048]{3,2,1,0:T(8,128)(2,1)} %bitcast.28) | data formatting | bytes 4194304 | tf_op jit(solution)/shard_map/all_to_all | solution.py:24
  109.5 0.0 copy-done.1
  109.5 8.2 %add_convert_fusion = bf16[1,10240,128]{2,1,0:T(8,128)(2,1)} fusion(f32[1,10240,128]{2,1,0:T(8,128)} %reshape.138, bf16[1,10240,128]{2,1,0:T(8,128)(2,1)S(1)} %copy-done.1, pred[10240]{0:T(1024)(128)(4,1)S(1)} %scatter_custom_fusion), kind=kLoop, calls=%fused_computation.5 | loop fusion | flops 5242880 | bytes 10496000 | tf_op jit(solution)/shard_map/convert_element_type | solution.py:41
  (5 shorter events, 0.0 us)
Async XLA Ops:
  0.6 68.9 %copy-start = (bf16[2048,640]{1,0:T(8,128)(2,1)S(1)}, bf16[2048,640]{1,0:T(8,128)(2,1)}, u32[]{:S(2)}) copy-start(bf16[2048,640]{1,0:T(8,128)(2,1)} %param.8) | copy-start | bytes 7864324
  6.5 14.1 %all-to-all-start.2 = ((s32[8,128,1]{1,2,0:T(1,128)}), s32[8,128,1]{1,2,0:T(1,128)S(1)}, u32[]{:S(2)}, u32[]{:S(2)}) async-start(s32[8,128,1]{1,2,0:T(1,128)} %bitcast.14), calls=%async_computation.2 | async-start | bytes 8192 | tf_op jit(solution)/shard_map/all_to_all | solution.py:56
  14.5 0.6 copy-start.2
  20.6 14.5 %all-to-all-start.3 = ((bf16[8,128,128]{2,1,0:T(8,128)(2,1)}), bf16[8,128,128]{2,1,0:T(8,128)(2,1)S(1)}, u32[]{:S(2)}, u32[]{:S(2)}) async-start(bf16[8,128,128]{2,1,0:T(8,128)(2,1)} %bitcast.23), calls=%async_computation.3 | async-start | bytes 524288 | tf_op jit(solution)/shard_map/all_to_all | solution.py:55
  35.1 37.6 %all-to-all-start.1 = ((bf16[128,4,2048]{0,2,1:T(8,128)(2,1)}), bf16[128,4,2048]{0,2,1:T(8,128)(2,1)}, u32[]{:S(2)}, u32[]{:S(2)}) async-start(bf16[128,4,2048]{0,2,1:T(8,128)(2,1)} %bitcast.42), calls=%async_computation.1 | async-start | bytes 4194304 | tf_op jit(solution)/shard_map/all_to_all | solution.py:17
  72.7 4.6 %copy-start.3 = (s32[1,8]{1,0:T(1,128)S(1)}, s32[1,8]{1,0:T(1,128)}, u32[]{:S(2)}) copy-start(s32[1,8]{1,0:T(1,128)} %param.11) | copy-start | bytes 100
  72.7 33.5 %all-to-all-start = ((bf16[4,128,2048]{2,1,0:T(8,128)(2,1)}), bf16[4,128,2048]{2,1,0:T(8,128)(2,1)}, u32[]{:S(2)}, u32[]{:S(2)}) async-start(bf16[4,128,2048]{2,1,0:T(8,128)(2,1)} %bitcast.44), calls=%async_computation | async-start | bytes 4194304 | tf_op jit(solution)/shard_map/all_to_all | solution.py:24
  106.2 3.3 %copy-start.1 = (bf16[1,10240,128]{2,1,0:T(8,128)(2,1)S(1)}, bf16[1,10240,128]{2,1,0:T(8,128)(2,1)}, u32[]{:S(2)}) copy-start(bf16[1,10240,128]{2,1,0:T(8,128)(2,1)} %param.9) | copy-start | bytes 7864324
where the time goes:
time: 119 us; the launch traced here: 118 us
  local copies, waits for them, and re-layouts  31.4 us (26%)
  blocking collectives  30 us (25%)
  starting transfers between devices  22.4 us (19%)
  other arithmetic  19.8 us (17%)
  matrix products  8.92 us (7%)
  waiting for transfers between devices  4.45 us (4%)
    all_gather x1, blocking collectives, per_device(): grads_all = lax.all_gather(key_grad, 'shard', axis=0, tiled=True)  30 us
    convert_element_type x1, other arithmetic, per_device(): (cleared + weight_grad.reshape(block_count, block_size)).astype(jnp.bfloa...  8.16 us
    all_to_all x1, starting transfers between devices, per_device(): lax.all_to_all(send_ids, 'rep', split_axis=0, concat_axis=0, tiled=True)  7.31 us
    scatter-add x1, other arithmetic, accumulate(): return blank.at[target].add(block_rows.astype(jnp.float32), mode='drop')  7.02 us
    reshape x1, local copies, waits for them, and re-layouts, per_device(): weight_grad.reshape(block_count, block_size)  6.47 us
    all_to_all x1, starting transfers between devices, per_device(): lax.all_to_all(send_rows, 'rep', split_axis=0, concat_axis=0, tiled=True)  6 us
    dot_general x1, matrix products, per_device(): lax.dot_general(act_cols, grads_all, (((0,), (0,)), ((), ())), preferred_...  5.78 us
    scatter x1, local copies, waits for them, and re-layouts, per_device(): jnp.zeros((replicas * capacity, block_size), jnp.bfloat16).at[place_at]  5.51 us
  transfers between devices with their start and end apart: 4, of which 1 were waited for; matrix products, arithmetic and copies ran while one was open for 36% of the time, Pallas kernels for 0%

commit v1 on v0

--- a/solution.py
+++ b/solution.py
@@ -2,6 +2,7 @@
 import jax.numpy as jnp
 from jax import lax
 from jax.sharding import PartitionSpec as P
+from jax.lax import all_to_all, axis_size
 
 
 def accumulate(block_rows, block_ids, own_start, own_len, region_max):
@@ -14,7 +15,13 @@
 
 def per_device(activ, key_grad, key_weight, feedback, kept, region_len):
     grads_all = lax.all_gather(key_grad, "shard", axis=0, tiled=True)
-    act_cols = lax.all_to_all(activ, "shard", split_axis=1, concat_axis=0, tiled=True)
+
+    def advance_files_by_axis(local):
+        opened = jnp.stack(jnp.split(local, axis_size("shard"), axis=1))
+        q_next = all_to_all(opened, "shard", 0, 0)
+        return jnp.concatenate(q_next, axis=0)
+
+    act_cols = advance_files_by_axis(activ)
     weight_grad = lax.dot_general(
         act_cols, grads_all, (((0,), (0,)), ((), ())), preferred_element_type=jnp.float32
     )

time: 119 us -> 116 us (0.975)
  local copies, waits for them, and re-layouts: 31.4 us -> 25 us
  waiting for transfers between devices: 4.45 us -> 6.2 us
  other arithmetic: 19.8 us -> 21.4 us
    unnamed x9 -> x8, local copies, waits for them, and re-layouts: 4.68 us -> 0.61 us
    all_to_all x1 -> x0, local copies, waits for them, and re-layouts: 3.94 us -> none  [per_device(): lax.all_to_all(activ, 'shard', split_axis=1, concat_axis=0, tiled=True)]
    another operation x0 -> x1, local copies, waits for them, and re-layouts: none -> 1.65 us  [advance_files_by_axis(): opened = jnp.stack(jnp.split(local, axis_size('shard'), axis=1))]
    another operation x1 -> x2, other arithmetic: 0.98 us -> 2.56 us  [the longest x1 1.58 us: advance_files_by_axis(): opened = jnp.stack(jnp.split(local, axis_size('shard'), axis=1))]
  transfers between devices with their start and end apart: 4 -> 4, of which waited for: 1 -> 2; matrix products, arithmetic and copies ran while one was open for 36% -> 33% of each run, Pallas kernels for 0% -> 0%
where the time goes in v1:
time: 116 us; the launch traced here: 115 us
  blocking collectives  30 us (26%)
  local copies, waits for them, and re-layouts  25 us (22%)
  starting transfers between devices  22.4 us (19%)
  other arithmetic  21.4 us (18%)
  matrix products  8.88 us (8%)
  waiting for transfers between devices  6.2 us (5%)
    all_gather x1, blocking collectives, per_device(): grads_all = lax.all_gather(key_grad, 'shard', axis=0, tiled=True)  30 us
    convert_element_type x1, other arithmetic, per_device(): (cleared + weight_grad.reshape(block_count, block_size)).astype(jnp.bfloa...  8.16 us
    all_to_all x1, starting transfers between devices, per_device(): lax.all_to_all(send_ids, 'rep', split_axis=0, concat_axis=0, tiled=True)  7.31 us
    scatter-add x1, other arithmetic, accumulate(): return blank.at[target].add(block_rows.astype(jnp.float32), mode='drop')  7.02 us
    reshape x1, local copies, waits for them, and re-layouts, per_device(): weight_grad.reshape(block_count, block_size)  6.48 us
    all_to_all x1, starting transfers between devices, per_device(): lax.all_to_all(send_rows, 'rep', split_axis=0, concat_axis=0, tiled=True)  6 us
    dot_general x1, matrix products, per_device(): lax.dot_general(act_cols, grads_all, (((0,), (0,)), ((), ())), preferred_...  5.73 us
    scatter x1, local copies, waits for them, and re-layouts, per_device(): jnp.zeros((replicas * capacity, block_size), jnp.bfloat16).at[place_at]  5.51 us
  transfers between devices with their start and end apart: 4, of which 2 were waited for; matrix products, arithmetic and copies ran while one was open for 33% of the time, Pallas kernels for 0%

profile of v1, /device:TPU:0, one launch (start us, length us, event | category | flops | bytes accessed | tf_op | source)
XLA Modules:
  0.0 114.6 jit_solution(15284508649840407491)
XLA Ops:
  0.6 0.0 copy-start
  0.6 1.0 reduce-window.4
  1.6 0.7 fusion.11
  2.3 0.8 convert_reduce_fusion.1
  3.1 0.3 convert_reduce_fusion
  3.3 3.2 %scatter_custom_fusion.1 = s32[1024]{0:T(1024)} fusion(s32[512]{0:T(512)S(1)} %bitcast.60, s32[512]{0:T(512)} %bitcast.58, s32[]{:T(128)} %constant.18.clone.1), kind=kCustom, calls=%fused_computation.31 | custom fusion | bytes 4608 | tf_op jit(solution)/shard_map/scatter | solution.py:60
  6.5 7.3 %all-to-all-start.2 = ((s32[8,128,1]{1,2,0:T(1,128)}), s32[8,128,1]{1,2,0:T(1,128)S(1)}, u32[]{:S(2)}, u32[]{:S(2)}) async-start(s32[8,128,1]{1,2,0:T(1,128)} %bitcast.16), calls=%async_computation.2 | async-start | bytes 8192 | tf_op jit(solution)/shard_map/all_to_all | solution.py:63
  13.8 0.7 compare_select_fusion.2
  14.5 0.0 copy-start.2
  14.5 0.6 copy-done.2
  15.1 5.5 %scatter_custom_fusion.2 = bf16[1024,128]{1,0:T(8,128)(2,1)} fusion(s32[512]{0:T(512)S(1)} %bitcast.61, bf16[]{:T(256)} %constant.12.clone.1, bf16[10240,128]{1,0:T(8,128)(2,1)} %bitcast.47, s32[1024]{0:T(1024)S(1)} %pad_clamp_fusion), kind=kCustom, calls=%fused_computation.18 | custom fusion | bytes 262656 | tf_op jit(solution)/shard_map/scatter | solution.py:58
  20.6 0.0 all-to-all-done.2
  20.6 6.0 %all-to-all-start.3 = ((bf16[8,128,128]{2,1,0:T(8,128)(2,1)}), bf16[8,128,128]{2,1,0:T(8,128)(2,1)S(1)}, u32[]{:S(2)}, u32[]{:S(2)}) async-start(bf16[8,128,128]{2,1,0:T(8,128)(2,1)} %bitcast.25), calls=%async_computation.3 | async-start | bytes 524288 | tf_op jit(solution)/shard_map/all_to_all | solution.py:62
  26.6 1.7 %slice_bitcast_fusion.3 = (bf16[1,128,2048]{2,1,0:T(8,128)(2,1)S(1)}, bf16[1,128,2048]{2,1,0:T(8,128)(2,1)S(1)}, bf16[1,128,2048]{2,1,0:T(8,128)(2,1)S(1)}, bf16[1,128,2048]{2,1,0:T(8,128)(2,1)S(1)}) fusion(bf16[128,8192]{1,0:T(8,128)(2,1)} %param.6), kind=kLoop, calls=%fused_computation.16 | loop fusion | bytes 4194304 | tf_op jit(solution)/shard_map/stack | solution.py:20
  28.3 1.6 %pad_maximum_fusion = bf16[4,128,2048]{2,1,0:T(8,128)(2,1)} fusion(bf16[1,128,2048]{2,1,0:T(8,128)(2,1)S(1)} %get-tuple-element.5, bf16[1,128,2048]{2,1,0:T(8,128)(2,1)S(1)} %get-tuple-element.6, bf16[1,128,2048]{2,1,0:T(8,128)(2,1)S(1)} %get-tuple-element.4, bf16[1,128,2048]{2,1,0:T(8,128)(2,1)S(1)} %get-tuple-element.3), kind=kLoop, calls=%fused_computation.7 | loop fusion | flops 3145728 | bytes 4194304 | tf_op jit(solution)/shard_map/stack | solution.py:20
  29.8 5.3 %all-to-all-done.3 = bf16[8,128,128]{2,1,0:T(8,128)(2,1)S(1)} async-done(((bf16[8,128,128]{2,1,0:T(8,128)(2,1)}), bf16[8,128,128]{2,1,0:T(8,128)(2,1)S(1)}, u32[]{:S(2)}, u32[]{:S(2)}) %all-to-all-start.3) | async-done | bytes 262176 | tf_op jit(solution)/shard_map/all_to_all | solution.py:62
  35.1 4.5 %all-to-all-start.1 = ((bf16[4,128,2048]{2,1,0:T(8,128)(2,1)}), bf16[4,128,2048]{2,1,0:T(8,128)(2,1)}, u32[]{:S(2)}, u32[]{:S(2)}) async-start(bf16[4,128,2048]{2,1,0:T(8,128)(2,1)} %pad_maximum_fusion), calls=%async_computation.1 | async-start | bytes 4194304 | tf_op jit(solution)/shard_map/all_to_all | solution.py:21
  39.6 30.0 %all_gather.3 = bf16[512,640]{1,0:T(8,128)(2,1)S(1)} all-gather(bf16[128,640]{1,0:T(8,128)(2,1)} %param.7), channel_id=1, replica_groups=mesh['rep'=8,'shard'=4] {'shard'}, dimensions={0}, use_global_device_ids=true | all-gather | bytes 819200 | tf_op jit(solution)/shard_map/all_gather | solution.py:17
  69.6 0.0 copy-done
  69.6 3.1 %convolution_convert_fusion = bf16[512,2048]{1,0:T(8,128)(2,1)} fusion(bf16[512,640]{1,0:T(8,128)(2,1)S(1)} %all_gather.3, bf16[2048,640]{1,0:T(8,128)(2,1)S(1)} %copy-done), kind=kOutput, calls=%fused_computation.6 | convolution fusion | flops 1343225856 | bytes 5373952 | tf_op jit(solution)/shard_map/dot_general | solution.py:28
  72.7 0.0 copy-start.3
  72.7 0.0 all-to-all-done.1
  72.7 4.6 %all-to-all-start = ((bf16[4,128,2048]{2,1,0:T(8,128)(2,1)}), bf16[4,128,2048]{2,1,0:T(8,128)(2,1)}, u32[]{:S(2)}, u32[]{:S(2)}) async-start(bf16[4,128,2048]{2,1,0:T(8,128)(2,1)} %bitcast.48), calls=%async_computation | async-start | bytes 4194304 | tf_op jit(solution)/shard_map/all_to_all | solution.py:31
  77.4 0.0 copy-done.3
  77.4 0.6 constant_dynamic-slice_fusion
  78.0 0.6 dynamic_slice.6
  78.6 0.5 broadcast.121
  79.1 2.6 %scatter_custom_fusion = pred[10240]{0:T(1024)(128)(4,1)S(1)} fusion(s32[512]{0:T(512)} %bitcast.55, pred[512]{0:T(512)(128)(4,1)} %broadcast.121, pred[]{:T(512)} %constant.13.clone.1), kind=kCustom, calls=%fused_computation.22 | custom fusion | bytes 10752 | tf_op jit(solution)/shard_map/scatter | solution.py:46
  81.7 0.7 broadcast_subtract_fusion
  82.3 0.6 compare_select_fusion
  82.9 7.0 %scatter_custom_fusion.3 = f32[1920,128]{1,0:T(8,128)} fusion(s32[1024]{0:T(1024)S(1)} %bitcast.59, bf16[1024,128]{1,0:T(8,128)(2,1)S(1)} %bitcast.50, f32[]{:T(128)} %constant.17.clone.1), kind=kCustom, calls=%fused_computation.11 | custom fusion | flops 262144 | bytes 1245188 | tf_op jit(solution)/shard_map/scatter-add | solution.py:13
  89.9 5.7 %fusion.12 = f32[2048,640]{1,0:T(8,128)} fusion(bf16[512,2048]{1,0:T(8,128)(2,1)} %bitcast.8, bf16[512,640]{1,0:T(8,128)(2,1)S(1)} %all_gather.3), kind=kOutput, calls=%fused_computation.38 | convolution fusion | flops 1342177280 | bytes 7995392 | tf_op jit(solution)/shard_map/dot_general | solution.py:25
  95.7 6.5 %reshape.139 = f32[1,10240,128]{2,1,0:T(8,128)} reshape(f32[2048,640]{1,0:T(8,128)} %fusion.12) | data formatting | bytes 10485760 | tf_op jit(solution)/shard_map/reshape | solution.py:48
  102.2 0.9 all-to-all-done
  103.1 0.0 copy-start.1
  103.1 3.3 %copy.17 = bf16[4,16,8,2048]{3,2,0,1:T(8,128)(2,1)} copy(bf16[4,16,8,2048]{3,2,1,0:T(8,128)(2,1)} %bitcast.30) | data formatting | bytes 4194304 | tf_op jit(solution)/shard_map/all_to_all | solution.py:31
  106.4 0.0 copy-done.1
  106.4 8.2 %add_convert_fusion = bf16[1,10240,128]{2,1,0:T(8,128)(2,1)} fusion(f32[1,10240,128]{2,1,0:T(8,128)} %reshape.139, bf16[1,10240,128]{2,1,0:T(8,128)(2,1)S(1)} %copy-done.1, pred[10240]{0:T(1024)(128)(4,1)S(1)} %scatter_custom_fusion), kind=kLoop, calls=%fused_computation.5 | loop fusion | flops 5242880 | bytes 10496000 | tf_op jit(solution)/shard_map/convert_element_type | solution.py:48
  (5 shorter events, 0.0 us)
Async XLA Ops:
  0.6 69.0 %copy-start = (bf16[2048,640]{1,0:T(8,128)(2,1)S(1)}, bf16[2048,640]{1,0:T(8,128)(2,1)}, u32[]{:S(2)}) copy-start(bf16[2048,640]{1,0:T(8,128)(2,1)} %param.8) | copy-start | bytes 7864324
  6.5 14.1 %all-to-all-start.2 = ((s32[8,128,1]{1,2,0:T(1,128)}), s32[8,128,1]{1,2,0:T(1,128)S(1)}, u32[]{:S(2)}, u32[]{:S(2)}) async-start(s32[8,128,1]{1,2,0:T(1,128)} %bitcast.16), calls=%async_computation.2 | async-start | bytes 8192 | tf_op jit(solution)/shard_map/all_to_all | solution.py:63
  14.5 0.6 copy-start.2
  20.6 14.5 %all-to-all-start.3 = ((bf16[8,128,128]{2,1,0:T(8,128)(2,1)}), bf16[8,128,128]{2,1,0:T(8,128)(2,1)S(1)}, u32[]{:S(2)}, u32[]{:S(2)}) async-start(bf16[8,128,128]{2,1,0:T(8,128)(2,1)} %bitcast.25), calls=%async_computation.3 | async-start | bytes 524288 | tf_op jit(solution)/shard_map/all_to_all | solution.py:62
  35.1 37.6 %all-to-all-start.1 = ((bf16[4,128,2048]{2,1,0:T(8,128)(2,1)}), bf16[4,128,2048]{2,1,0:T(8,128)(2,1)}, u32[]{:S(2)}, u32[]{:S(2)}) async-start(bf16[4,128,2048]{2,1,0:T(8,128)(2,1)} %pad_maximum_fusion), calls=%async_computation.1 | async-start | bytes 4194304 | tf_op jit(solution)/shard_map/all_to_all | solution.py:21
  72.7 4.6 %copy-start.3 = (s32[1,8]{1,0:T(1,128)S(1)}, s32[1,8]{1,0:T(1,128)}, u32[]{:S(2)}) copy-start(s32[1,8]{1,0:T(1,128)} %param.11) | copy-start | bytes 100
  72.7 30.3 %all-to-all-start = ((bf16[4,128,2048]{2,1,0:T(8,128)(2,1)}), bf16[4,128,2048]{2,1,0:T(8,128)(2,1)}, u32[]{:S(2)}, u32[]{:S(2)}) async-start(bf16[4,128,2048]{2,1,0:T(8,128)(2,1)} %bitcast.48), calls=%async_computation | async-start | bytes 4194304 | tf_op jit(solution)/shard_map/all_to_all | solution.py:31
  103.1 3.3 %copy-start.1 = (bf16[1,10240,128]{2,1,0:T(8,128)(2,1)S(1)}, bf16[1,10240,128]{2,1,0:T(8,128)(2,1)}, u32[]{:S(2)}) copy-start(bf16[1,10240,128]{2,1,0:T(8,128)(2,1)} %param.9) | copy-start | bytes 7864324
